TPU v7x, 256 devices: a whole 4x4x8 slice. The times are simulated.
256 devices in a mesh: rep: 2 (over core), dp: 128 (over x, y, z).
Axes of the slice: x: 4, y: 4, z: 8, core: 2. Of those that a mesh axis runs over, the one named last changes fastest.
Arguments:
- x: bfloat16 [256, 2048, 896], P(('rep', 'dp')), parts along dimension 0
- dy: bfloat16 [256, 2048, 896], P(('rep', 'dp')), parts along dimension 0
- w_gate: bfloat16 [2, 896, 2560], replicated
- w_up: bfloat16 [2, 896, 2560], replicated
- w_down: bfloat16 [2, 2560, 896], replicated
- m_w_gate: float32 [2, 896, 2560], P(None, 'dp')
- m_w_up: float32 [2, 896, 2560], P(None, 'dp')
- m_w_down: float32 [2, 2560, 896], P(None, 'dp')
- v_w_gate: float32 [2, 896, 2560], P(None, 'dp')
- v_w_up: float32 [2, 896, 2560], P(None, 'dp')
- v_w_down: float32 [2, 2560, 896], P(None, 'dp')
Outputs:
- output 1: bfloat16 [4, 896, 2560], P('rep'), parts along dimension 0
- output 2: bfloat16 [4, 896, 2560], P('rep'), parts along dimension 0
- output 3: bfloat16 [4, 2560, 896], P('rep'), parts along dimension 0
- output 4: float32 [4, 896, 2560], P('rep', 'dp'), parts along dimension 0
- output 5: float32 [4, 896, 2560], P('rep', 'dp'), parts along dimension 0
- output 6: float32 [4, 2560, 896], P('rep', 'dp'), parts along dimension 0
- output 7: float32 [4, 896, 2560], P('rep', 'dp'), parts along dimension 0
- output 8: float32 [4, 896, 2560], P('rep', 'dp'), parts along dimension 0
- output 9: float32 [4, 2560, 896], P('rep', 'dp'), parts along dimension 0
There are 2 independent parts. A program takes and returns all parts, laid end to end along the dimension named above; an argument that names none is the same for every part.
All inputs are finite; a program needn't handle non-finite values.
Results may differ from a plain program's by a relative error of at most 0.022.
Values are sent between devices in bfloat16 or wider.
A program may use at most 768 MiB of HBM per device.

v0:
```python
import jax
import jax.numpy as jnp
from jax import lax

NAMES = ("w_gate", "w_up", "w_down")


def matmul(a, w):
    return jnp.dot(a, w, preferred_element_type=jnp.float32).astype(jnp.bfloat16)


def normed(h):
    wide = h.astype(jnp.float32)
    scale = lax.rsqrt(jnp.mean(wide**2, -1, keepdims=True) + 1e-6)
    return (wide * scale).astype(jnp.bfloat16)


def layer(h, w):
    a = normed(h)
    gate = jnp.dot(a, w["w_gate"], preferred_element_type=jnp.float32)
    up = jnp.dot(a, w["w_up"], preferred_element_type=jnp.float32)
    return h + matmul((jax.nn.silu(gate) * up).astype(jnp.bfloat16), w["w_down"])


def adamw(w, m, v, g):
    m = 0.9 * m + 0.1 * g
    v = 0.95 * v + 0.05 * g * g
    step = m * lax.rsqrt(v + 1e-8) + 0.1 * w
    return (w - 0.02 * step).astype(jnp.bfloat16), m, v


def stack(weights, h):
    for number in range(weights["w_gate"].shape[0]):
        h = layer(h, {name: w[number] for name, w in weights.items()})
    return h


def solution(mesh):
    groups = mesh.shape["rep"]

    def step(x, dy, *arrays):
        weights, m, v = (arrays[i : i + 3] for i in (0, 3, 6))
        x, dy = (t.reshape(groups, -1, *t.shape[1:]) for t in (x, dy))

        def of_a_group(x, dy):
            _, back = jax.vjp(lambda w: stack(w, x), dict(zip(NAMES, weights, strict=True)))
            by_weights = back(dy)[0]
            gradients = [by_weights[name].astype(jnp.float32) for name in NAMES]
            new = [adamw(w.astype(jnp.float32), m, v, g) for w, m, v, g in zip(weights, m, v, gradients, strict=True)]
            return tuple(one[which] for which in range(3) for one in new)

        return tuple(t.reshape(-1, *t.shape[2:]) for t in jax.vmap(of_a_group)(x, dy))

    return step
```

profile of v0, /device:TPU:2, one launch (start us, length us, event | category | flops | bytes accessed | tf_op | source)
XLA Modules:
  0.0 2186.5 jit_solution(5889202314406708029)
XLA Ops:
  16.2 14.2 fusion.71
  30.4 22.5 %fusion.69 = f32[2048,2560]{1,0:T(8,128)} fusion(bf16[2,896,2560]{2,1,0:T(8,128)(2,1)} %param.3, bf16[1,2048,896]{2,1,0:T(8,128)(2,1)} %param.2, f32[2048]{0:T(1024)S(1)} %add_rsqrt_fusion), kind=kOutput, calls=%fused_computation.77 | convolution fusion | flops 9400745984 | bytes 29237248 | tf_op jit(solution)/vmap(jvp())/dot_general | solution.py:21
  53.0 15.3 fusion.30
  68.3 15.1 fusion.43
  84.1 17.6 fusion.60
  101.7 17.7 fusion.63
  119.5 15.6 convolution_convert_fusion.1
  141.2 22.3 %fusion.46 = f32[1,2560,896]{2,1,0:T(8,128)} fusion(f32[2048,2560]{1,0:T(8,128)} %fusion.63, f32[2048,2560]{1,0:T(8,128)} %fusion.60, bf16[1,2048,896]{2,1,0:T(8,128)(2,1)} %param.5), kind=kOutput, calls=%fused_computation.60 | convolution fusion | flops 9426698240 | bytes 54788096 | tf_op jit(solution)/vmap(transpose(jvp()))/dot_general | solution.py:9
  163.5 22.5 %fusion.10 = bf16[2048,2560]{1,0:T(8,128)(2,1)} fusion(f32[2048,2560]{1,0:T(8,128)} %fusion.60, f32[2048,2560]{1,0:T(8,128)} %fusion.63, bf16[2048,2560]{1,0:T(8,128)(2,1)} %convolution_convert_fusion.1), kind=kLoop, calls=%fused_computation.11 | loop fusion | flops 62914560 | bytes 62914560
  186.0 15.1 fusion.58
  201.2 20.6 fusion.45
  229.1 15.4 convolution_bitcast_fusion
  245.8 748.0 %all-reduce.19 = (bf16[1,2560,896]{2,1,0:T(8,128)(2,1)}, bf16[1,2560,896]{2,1,0:T(8,128)(2,1)}) all-reduce(f32[1,2560,896]{2,1,0:T(8,128)} %convolution_bitcast_fusion, f32[1,2560,896]{2,1,0:T(8,128)} %fusion.46), channel_id=18, replica_groups=[2,128]<=[256], use_global_device_ids=true, to_apply=%add.5.clone.clone | all-reduce | flops 4587520 | bytes 27525120
  997.9 16.6 convolution_convert_fusion
  1014.5 14.5 convolution_bitcast_fusion.1
  1029.0 19.6 fusion.49
  1048.6 19.2 fusion.55
  1067.8 26.4 %fusion.52 = f32[1,896,2560]{2,1,0:T(8,128)} fusion(f32[2048,2560]{1,0:T(8,128)} %copy-done, f32[2048,2560]{1,0:T(8,128)} %fusion.69, bf16[2048,2560]{1,0:T(8,128)(2,1)} %convolution_convert_fusion, bf16[1,2048,896]{1,2,0:T(8,128)(2,1)} %copy.15, f32[2048]{0:T(1024)S(1)} %copy-done.39), kind=kOutput, calls=%fused_computation.62 | convolution fusion | flops 9458417664 | bytes 65282048 | tf_op jit(solution)/vmap(transpose(jvp()))/dot_general | solution.py:20
  1094.2 507.7 %fusion.141 = (f32[8,2560]{1,0:T(8,128)S(1)}, f32[8,2560]{1,0:T(8,128)S(1)}, f32[8,2560]{1,0:T(8,128)S(1)}, f32[8,2560]{1,0:T(8,128)S(1)}) fusion(f32[1,896,2560]{2,1,0:T(8,128)} %fusion.52, f32[1,896,2560]{2,1,0:T(8,128)} %convolution_bitcast_fusion.1, f32[1,896,2560]{2,1,0:T(8,128)} %fusion.55, f32[1,896,2560]{2,1,0:T(8,128)} %fusion.49), kind=kCustom, calls=%all-reduce-scatter.4 | all-reduce-scatter fusion | flops 10485761 | bytes 37028864
  1608.0 10.7 collective-permute-start.63
  1623.0 35.9 %collective-permute-done.15 = bf16[7,2560]{1,0:T(8,128)(2,1)S(1)} collective-permute-done((bf16[7,2560]{1,0:T(8,128)(2,1)S(1)}, bf16[7,2560]{1,0:T(8,128)(2,1)S(1)}, u32[]{:S(2)}, u32[]{:S(2)}) %collective-permute-start.15) | collective-permute-done | bytes 35872
  1660.8 11.3 collective-permute-start.10
  1672.2 35.1 %collective-permute-start.11 = (bf16[8,2560]{1,0:T(8,128)(2,1)S(1)}, bf16[8,2560]{1,0:T(8,128)(2,1)S(1)}, u32[]{:S(2)}, u32[]{:S(2)}) collective-permute-start(bf16[8,2560]{1,0:T(8,128)(2,1)S(1)} %convert.166), channel_id=1, source_target_pairs={{0,12},{1,13},{2,14},{3,15},{4,16},{5,17},{6,18},{7,19},{8,20},{9,... | collective-permute-start | bytes 122888
  1707.3 7.9 collective-permute-start.12
  1715.2 7.1 collective-permute-start.13
  1885.6 13.3 concatenate.2
  1898.9 14.0 concatenate.3
  1920.7 8.4 copy.27
  1929.1 115.3 %all-gather.10.cloned.1.call-done = bf16[1,2,896,2560]{3,1,0,2:T(2,128)(2,1)} async-done(((bf16[1,2,7,2560]{3,1,0,2:T(2,128)(2,1)}), bf16[1,2,896,2560]{3,1,0,2:T(2,128)(2,1)}) %all-gather.10.cloned.1.call-update) | async-done | bytes 9175056 | tf_op jit(solution)/reshape | solution.py:52
  2044.4 8.7 copy.25
  2053.1 117.8 %all-gather.12.cloned.1.call-done = bf16[1,2,896,2560]{3,1,0,2:T(2,128)(2,1)} async-done(((bf16[1,2,7,2560]{3,1,0,2:T(2,128)(2,1)}), bf16[1,2,896,2560]{3,1,0,2:T(2,128)(2,1)}) %all-gather.12.cloned.1.call-update) | async-done | bytes 9175056 | tf_op jit(solution)/reshape | solution.py:52
  2170.8 8.7 copy.26
  (253 shorter events, 208.5 us)
Async XLA Ops:
  7.2 1913.5 %all-gather.14.cloned.1.call-start = ((), (), s32[]{:S(2)}) async-start(), calls=%async_computation.2 | async-start | bytes 9246720 | tf_op jit(solution)/reshape | solution.py:52
  997.8 1046.5 %all-gather.10.cloned.1.call-start = ((), (), s32[]{:S(2)}) async-start(), calls=%async_computation | async-start | bytes 9246720 | tf_op jit(solution)/reshape | solution.py:52
  1602.0 56.9 %collective-permute-start.15 = (bf16[7,2560]{1,0:T(8,128)(2,1)S(1)}, bf16[7,2560]{1,0:T(8,128)(2,1)S(1)}, u32[]{:S(2)}, u32[]{:S(2)}) collective-permute-start(bf16[7,2560]{1,0:T(8,128)(2,1)S(1)} %slice.24), channel_id=1, source_target_pairs={{0,16},{1,17},{2,18},{3,19},{4,20},{5,21},{6,22},{7,23},{8,24},{9,... | collective-permute-start | bytes 107528
  1604.1 56.7 %collective-permute-start.31 = (bf16[7,2560]{1,0:T(8,128)(2,1)S(1)}, bf16[7,2560]{1,0:T(8,128)(2,1)S(1)}, u32[]{:S(2)}, u32[]{:S(2)}) collective-permute-start(bf16[7,2560]{1,0:T(8,128)(2,1)S(1)} %slice.25), channel_id=1, source_target_pairs={{0,16},{1,17},{2,18},{3,19},{4,20},{5,21},{6,22},{7,23},{8,24},{9,... | collective-permute-start | bytes 107528
  1606.0 66.1 %collective-permute-start.47 = (bf16[7,2560]{1,0:T(8,128)(2,1)S(1)}, bf16[7,2560]{1,0:T(8,128)(2,1)S(1)}, u32[]{:S(2)}, u32[]{:S(2)}) collective-permute-start(bf16[7,2560]{1,0:T(8,128)(2,1)S(1)} %slice.26), channel_id=1, source_target_pairs={{0,16},{1,17},{2,18},{3,19},{4,20},{5,21},{6,22},{7,23},{8,24},{9,... | collective-permute-start | bytes 107528
  1608.0 99.3 %collective-permute-start.63 = (bf16[7,2560]{1,0:T(8,128)(2,1)S(1)}, bf16[7,2560]{1,0:T(8,128)(2,1)S(1)}, u32[]{:S(2)}, u32[]{:S(2)}) collective-permute-start(bf16[7,2560]{1,0:T(8,128)(2,1)S(1)} %slice.27), channel_id=1, source_target_pairs={{0,16},{1,17},{2,18},{3,19},{4,20},{5,21},{6,22},{7,23},{8,24},{9,... | collective-permute-start | bytes 107528
  1618.7 96.6 %collective-permute-start = (bf16[8,2560]{1,0:T(8,128)(2,1)S(1)}, bf16[8,2560]{1,0:T(8,128)(2,1)S(1)}, u32[]{:S(2)}, u32[]{:S(2)}) collective-permute-start(bf16[8,2560]{1,0:T(8,128)(2,1)S(1)} %convert.166), channel_id=1, source_target_pairs={{0,1},{1,2},{2,3},{3,4},{4,5},{5,6},{6,7},{7,8},{8,9},{9,10},{10,1... | collective-permute-start | bytes 122888
  1658.9 63.5 %collective-permute-start.1 = (bf16[8,2560]{1,0:T(8,128)(2,1)S(1)}, bf16[8,2560]{1,0:T(8,128)(2,1)S(1)}, u32[]{:S(2)}, u32[]{:S(2)}) collective-permute-start(bf16[8,2560]{1,0:T(8,128)(2,1)S(1)} %convert.166), channel_id=1, source_target_pairs={{0,2},{1,3},{2,4},{3,5},{4,6},{5,7},{6,8},{7,9},{8,10},{9,11},{10,... | collective-permute-start | bytes 122888
  1660.8 63.9 %collective-permute-start.10 = (bf16[8,2560]{1,0:T(8,128)(2,1)S(1)}, bf16[8,2560]{1,0:T(8,128)(2,1)S(1)}, u32[]{:S(2)}, u32[]{:S(2)}) collective-permute-start(bf16[8,2560]{1,0:T(8,128)(2,1)S(1)} %convert.166), channel_id=1, source_target_pairs={{0,11},{1,12},{2,13},{3,14},{4,15},{5,16},{6,17},{7,18},{8,19},{9,... | collective-permute-start | bytes 122888
  1672.2 58.4 %collective-permute-start.11 = (bf16[8,2560]{1,0:T(8,128)(2,1)S(1)}, bf16[8,2560]{1,0:T(8,128)(2,1)S(1)}, u32[]{:S(2)}, u32[]{:S(2)}) collective-permute-start(bf16[8,2560]{1,0:T(8,128)(2,1)S(1)} %convert.166), channel_id=1, source_target_pairs={{0,12},{1,13},{2,14},{3,15},{4,16},{5,17},{6,18},{7,19},{8,20},{9,... | collective-permute-start | bytes 122888
  1707.3 29.6 %collective-permute-start.12 = (bf16[8,2560]{1,0:T(8,128)(2,1)S(1)}, bf16[8,2560]{1,0:T(8,128)(2,1)S(1)}, u32[]{:S(2)}, u32[]{:S(2)}) collective-permute-start(bf16[8,2560]{1,0:T(8,128)(2,1)S(1)} %convert.166), channel_id=1, source_target_pairs={{0,13},{1,14},{2,15},{3,16},{4,17},{5,18},{6,19},{7,20},{8,21},{9,... | collective-permute-start | bytes 122888
  1715.2 27.8 %collective-permute-start.13 = (bf16[8,2560]{1,0:T(8,128)(2,1)S(1)}, bf16[8,2560]{1,0:T(8,128)(2,1)S(1)}, u32[]{:S(2)}, u32[]{:S(2)}) collective-permute-start(bf16[8,2560]{1,0:T(8,128)(2,1)S(1)} %convert.166), channel_id=1, source_target_pairs={{0,14},{1,15},{2,16},{3,17},{4,18},{5,19},{6,20},{7,21},{8,22},{9,... | collective-permute-start | bytes 122888
  1722.4 22.6 %collective-permute-start.14 = (bf16[8,2560]{1,0:T(8,128)(2,1)S(1)}, bf16[8,2560]{1,0:T(8,128)(2,1)S(1)}, u32[]{:S(2)}, u32[]{:S(2)}) collective-permute-start(bf16[8,2560]{1,0:T(8,128)(2,1)S(1)} %convert.166), channel_id=1, source_target_pairs={{0,15},{1,16},{2,17},{3,18},{4,19},{5,20},{6,21},{7,22},{8,23},{9,... | collective-permute-start | bytes 122888
  1724.7 23.9 %collective-permute-start.2 = (bf16[8,2560]{1,0:T(8,128)(2,1)S(1)}, bf16[8,2560]{1,0:T(8,128)(2,1)S(1)}, u32[]{:S(2)}, u32[]{:S(2)}) collective-permute-start(bf16[8,2560]{1,0:T(8,128)(2,1)S(1)} %convert.166), channel_id=1, source_target_pairs={{0,3},{1,4},{2,5},{3,6},{4,7},{5,8},{6,9},{7,10},{8,11},{9,12},{10... | collective-permute-start | bytes 122888
  1730.5 20.1 collective-permute-start.3
  1752.7 16.6 collective-permute-start.9
  1754.6 19.2 collective-permute-start.16
  1757.9 19.3 collective-permute-start.17
  1761.3 17.8 collective-permute-start.18
  1792.3 16.0 collective-permute-start.29
  1794.6 18.4 collective-permute-start.30
  1797.1 17.7 collective-permute-start.32
  1800.4 16.8 collective-permute-start.33
  1803.8 15.7 collective-permute-start.34
  1836.3 18.4 collective-permute-start.46
  1838.9 17.8 collective-permute-start.48
  1868.2 30.7 %collective-permute-start.58 = (bf16[8,2560]{1,0:T(8,128)(2,1)}, bf16[8,2560]{1,0:T(8,128)(2,1)}, u32[]{:S(2)}, u32[]{:S(2)}) collective-permute-start(bf16[8,2560]{1,0:T(8,128)(2,1)} %convert.165), channel_id=1, source_target_pairs={{0,11},{1,12},{2,13},{3,14},{4,15},{5,16},{6,17},{7,18},{8,19},{9,... | collective-permute-start | bytes 122888
  1870.1 28.8 %collective-permute-start.59 = (bf16[8,2560]{1,0:T(8,128)(2,1)}, bf16[8,2560]{1,0:T(8,128)(2,1)}, u32[]{:S(2)}, u32[]{:S(2)}) collective-permute-start(bf16[8,2560]{1,0:T(8,128)(2,1)} %convert.165), channel_id=1, source_target_pairs={{0,12},{1,13},{2,14},{3,15},{4,16},{5,17},{6,18},{7,19},{8,20},{9,... | collective-permute-start | bytes 122888
  1872.8 26.1 %collective-permute-start.60 = (bf16[8,2560]{1,0:T(8,128)(2,1)}, bf16[8,2560]{1,0:T(8,128)(2,1)}, u32[]{:S(2)}, u32[]{:S(2)}) collective-permute-start(bf16[8,2560]{1,0:T(8,128)(2,1)} %convert.165), channel_id=1, source_target_pairs={{0,13},{1,14},{2,15},{3,16},{4,17},{5,18},{6,19},{7,20},{8,21},{9,... | collective-permute-start | bytes 122888
  1874.8 24.1 %collective-permute-start.61 = (bf16[8,2560]{1,0:T(8,128)(2,1)}, bf16[8,2560]{1,0:T(8,128)(2,1)}, u32[]{:S(2)}, u32[]{:S(2)}) collective-permute-start(bf16[8,2560]{1,0:T(8,128)(2,1)} %convert.165), channel_id=1, source_target_pairs={{0,14},{1,15},{2,16},{3,17},{4,18},{5,19},{6,20},{7,21},{8,22},{9,... | collective-permute-start | bytes 122888
  1877.5 21.4 collective-permute-start.62
  1915.3 255.5 %all-gather.12.cloned.1.call-start = ((), (), s32[]{:S(2)}) async-start(), calls=%async_computation.1 | async-start | bytes 9246720 | tf_op jit(solution)/reshape | solution.py:52
  (79 other events, 3674.1 us)
Sparse Core Ops, SparseCore 0:
  998.0 234.7 all-gather.13
  1915.5 128.8 all-gather.9
  2048.1 122.7 all-gather.11
where the time goes:
time: 2200 us; the launch traced here: 2190 us
  blocking collectives  1260 us (57%)
  matrix products  273 us (12%)
  waiting for transfers between devices  272 us (12%)
  starting transfers between devices  237 us (11%)
  local copies, waits for them, and re-layouts  79.8 us (4%)
  other arithmetic  51.9 us (2%)
    unnamed x2, blocking collectives  1260 us
    unnamed x64, starting transfers between devices  237 us
    reshape x3, waiting for transfers between devices, step(): t.reshape(-1, *t.shape[2:])  233 us
    dot_general x5, matrix products, layer(): up = jnp.dot(a, w['w_up'], preferred_element_type=jnp.float32)  99.7 us
    dot_general x5, matrix products, layer(): gate = jnp.dot(a, w['w_gate'], preferred_element_type=jnp.float32)  87.8 us
    dot_general x5, matrix products, matmul(): jnp.dot(a, w, preferred_element_type=jnp.float32).astype(jnp.bfloat16)  85 us
    unnamed x108, local copies, waits for them, and re-layouts  76.7 us
    unnamed x8, other arithmetic  45 us
  transfers between devices with their start and end apart: 67, of which 10 were waited for; matrix products, arithmetic and copies ran while one was open for 30% of the time, Pallas kernels for 0%

commit v1 on v0

v1 whole, which is shorter than its diff:
```python
import functools

import jax
import jax.numpy as jnp
from jax import lax
from jax.experimental import pallas as pl
from jax.experimental.pallas import tpu as pltpu
from jax.sharding import PartitionSpec as P

NX, NY, NZ = 4, 4, 8
D, FF = 896, 2560
F32, BF16 = jnp.float32, jnp.bfloat16

GATE = dict(r=7, rp=8, widths=(640, 640, 1280))
UP = dict(r=7, rp=8, widths=(768, 768, 1024))
DOWN1 = dict(r=20, rp=24, widths=(512, 384, 0))
DOWN0 = dict(r=20, rp=24, widths=(384, 512, 0))
CHUNKS = (
    ("w_down", 1, DOWN1, 1, "x"),
    ("w_gate", 1, GATE, -1, "x"),
    ("w_up", 1, UP, 1, "y"),
    ("w_down", 0, DOWN0, -1, "x"),
    ("w_gate", 0, GATE, 1, "x"),
    ("w_up", 0, UP, -1, "y"),
)


class Torus:
    def __init__(self):
        self.size = {"x": NX, "y": NY, "z": NZ}
        dp = lax.axis_index("dp")
        self.rep = lax.axis_index("rep")
        self.me = {"x": dp // (NY * NZ), "y": lax.rem(dp // NZ, NY), "z": lax.rem(dp, NZ)}

    def shifted(self, axis, by):
        return lax.rem(self.me[axis] + by + self.size[axis], self.size[axis])

    def neighbour(self, axis, by):
        place = dict(self.me)
        place[axis] = self.shifted(axis, by)
        return (self.rep, (place["x"] * NY + place["y"]) * NZ + place["z"])

    def barrier(self):
        sem = pltpu.get_barrier_semaphore()
        count = 0
        for axis in "xyz":
            for by in (1, -1):
                if self.size[axis] > (1 if by == 1 else 2):
                    pl.semaphore_signal(sem, inc=1, device_id=self.neighbour(axis, by), device_id_type=pl.DeviceIdType.MESH)
                    count += 1
        pl.semaphore_wait(sem, count)


class Ring:
    def __init__(self, torus, axis, sign, send, recv, base):
        n = torus.size[axis]
        self.torus, self.axis, self.n = torus, axis, n
        self.signs = (sign, -sign)
        self.hops = (n // 2, n - 1 - n // 2)
        self.send, self.recv, self.base = send, recv, base
        self.started = []

    def slot(self, flow, hop):
        return hop - 1 + (self.hops[0] if flow else 0)

    def copy(self, flow, hop, src, dst):
        at = self.base + self.slot(flow, hop)
        return pltpu.make_async_remote_copy(
            src_ref=src,
            dst_ref=dst,
            send_sem=self.send.at[at],
            recv_sem=self.recv.at[at],
            device_id=self.torus.neighbour(self.axis, self.signs[flow]),
            device_id_type=pl.DeviceIdType.MESH,
        )

    def start(self, flow, hop, src, dst):
        copy = self.copy(flow, hop, src, dst)
        copy.start()
        self.started.append(copy)

    def drain(self):
        for copy in self.started:
            copy.wait_send()


def total(into, terms):
    *lead, rows, columns = into.shape
    block = max(b for b in range(8, rows + 1, 8) if rows % b == 0 and (b == 8 or b * columns <= 40 * 1024))
    per = rows // block
    count = per
    for n in lead:
        count *= n

    def step(i, carry):
        at = []
        if per > 1:
            at = [pl.ds(pl.multiple_of(lax.rem(i, per) * block, block), block)]
            i = i // per
        else:
            at = [slice(None)]
        for n in reversed(lead):
            at.insert(0, lax.rem(i, n))
            i = i // n
        at = tuple(at)
        value = terms[0][at].astype(F32)
        for term in terms[1:]:
            value = value + term[at].astype(F32)
        into[at] = value.astype(into.dtype)
        return carry

    if count == 1:
        step(0, 0)
    else:
        lax.fori_loop(0, count, step, 0)


class SumOver:
    def __init__(self, ring, piece, terms, got):
        self.ring, self.piece, self.terms, self.got = ring, piece, terms, got

    def shard(self, flow, hop):
        return self.ring.torus.shifted(self.ring.axis, self.ring.signs[flow] * (self.ring.hops[flow] - hop))

    def pass_on(self, flow, hop):
        ring = self.ring
        if hop >= ring.hops[flow]:
            return
        i = self.shard(flow, hop)
        piece, terms = self.piece(i), list(self.terms(i))
        if hop:
            got = self.got.at[ring.slot(flow, hop)]
            ring.copy(flow, hop, got, got).wait_recv()
            terms.append(got)
        if len(terms) > 1 or terms[0] is not piece:
            total(piece, terms)
        ring.start(flow, hop + 1, piece, self.got.at[ring.slot(flow, hop + 1)])

    def step(self, hop):
        for flow in (0, 1):
            self.pass_on(flow, hop)

    def arrived(self):
        slots = []
        for flow in (0, 1):
            if self.ring.hops[flow]:
                slot = self.ring.slot(flow, self.ring.hops[flow])
                self.ring.copy(flow, self.ring.hops[flow], self.got.at[slot], self.got.at[slot]).wait_recv()
                slots.append(slot)
        return slots


def sums_xy(torus, first, second, own, got, wide, pieces, out, sign, sems, r, rp):
    me = torus.me
    flat, padded = wide
    send, recv, base = sems
    n1, n2 = torus.size[first], torus.size[second]
    rings = (
        Ring(torus, first, sign, send, recv, base),
        Ring(torus, second, sign, send, recv, base + n1 - 1),
        Ring(torus, "z", sign, send, recv, base + n1 + n2 - 2),
    )
    if first == "x":
        of_first, of_both = (lambda i: own.at[i]), (lambda j: own.at[me["x"], j])
    else:
        of_first, of_both = (lambda i: own.at[:, i]), (lambda j: own.at[j, me["y"]])
    one = SumOver(rings[0], of_first, lambda i: [of_first(i)], got[0])
    one.terms = None
    state = {}

    def first_pass(hop):
        for flow in (0, 1):
            if hop >= rings[0].hops[flow]:
                continue
            i = one.shard(flow, hop)
            piece = of_first(i)
            if hop:
                arrived = got[0].at[rings[0].slot(flow, hop)]
                rings[0].copy(flow, hop, arrived, arrived).wait_recv()
                total(piece, [piece, arrived])
            rings[0].start(flow, hop + 1, piece, got[0].at[rings[0].slot(flow, hop + 1)])

    def second_start():
        slots = one.arrived()
        terms = lambda j: [of_both(j)] + [got[0].at[s, j] for s in slots]
        state["two"] = SumOver(rings[1], of_both, terms, got[1])
        state["terms"] = terms
        state["two"].step(0)

    def third_start():
        slots = state["two"].arrived()
        total(flat, state["terms"](me[second]) + [got[1].at[s] for s in slots])
        for z in range(NZ):
            padded[z, 0:r, :] = flat[z * r : (z + 1) * r, :]
        state["three"] = SumOver(rings[2], lambda k: pieces.at[k], lambda k: [padded.at[k]], got[2])
        state["three"].step(0)

    def finish():
        slots = state["three"].arrived()
        total(out, [padded.at[me["z"]]] + [got[2].at[s] for s in slots])
        for ring in rings:
            ring.drain()

    stages = [functools.partial(first_pass, h) for h in range(max(1, n1 // 2))]
    stages.append(second_start)
    stages += [functools.partial(lambda h: state["two"].step(h), h) for h in range(1, n2 // 2)]
    stages.append(third_start)
    stages += [functools.partial(lambda h: state["three"].step(h), h) for h in range(1, NZ // 2)]
    stages.append(finish)
    return stages


def sums_z(torus, second, own, got, out, sign, sems):
    me = torus.me
    third = "y" if second == "x" else "x"
    send, recv, base = sems
    n2, n3 = torus.size[second], torus.size[third]
    rings = (
        Ring(torus, "z", sign, send, recv, base),
        Ring(torus, second, sign, send, recv, base + NZ - 1),
        Ring(torus, third, sign, send, recv, base + NZ + n2 - 2),
    )
    of_one = lambda k: own.at[:, :, k]
    if second == "x":
        own_two, got_two = (lambda i: own.at[i, :, me["z"]]), (lambda s, i: got[0].at[s, i])
        own_three = lambda j: own.at[me["x"], j, me["z"]]
        got_three = lambda s, j: got[0].at[s, me["x"], j]
    else:
        own_two, got_two = (lambda j: own.at[:, j, me["z"]]), (lambda s, j: got[0].at[s, :, j])
        own_three = lambda i: own.at[i, me["y"], me["z"]]
        got_three = lambda s, i: got[0].at[s, i, me["y"]]
    one = SumOver(rings[0], None, None, got[0])
    state = {}

    def first_pass(hop):
        for flow in (0, 1):
            if hop >= rings[0].hops[flow]:
                continue
            piece = of_one(one.shard(flow, hop))
            if hop:
                arrived = got[0].at[rings[0].slot(flow, hop)]
                rings[0].copy(flow, hop, arrived, arrived).wait_recv()
                total(piece, [piece, arrived])
            rings[0].start(flow, hop + 1, piece, got[0].at[rings[0].slot(flow, hop + 1)])

    def second_start():
        state["one"] = one.arrived()
        terms = lambda i: [own_two(i)] + [got_two(s, i) for s in state["one"]]
        state["two"] = SumOver(rings[1], own_two, terms, got[1])
        state["two"].step(0)

    def third_start():
        slots = state["two"].arrived()
        terms = lambda j: [own_three(j)] + [got_three(s, j) for s in state["one"]] + [got[1].at[s, j] for s in slots]
        state["terms"] = terms
        state["three"] = SumOver(rings[2], own_three, terms, got[2])
        state["three"].step(0)

    def finish():
        slots = state["three"].arrived()
        total(out, state["terms"](me[third]) + [got[2].at[s] for s in slots])
        for ring in rings:
            ring.drain()

    stages = [functools.partial(first_pass, h) for h in range(max(1, NZ // 2))]
    stages.append(second_start)
    stages += [functools.partial(lambda h: state["two"].step(h), h) for h in range(1, n2 // 2)]
    stages.append(third_start)
    stages += [functools.partial(lambda h: state["three"].step(h), h) for h in range(1, n3 // 2)]
    stages.append(finish)
    return stages


HOPS = (NX - 1) + (NY - 1) + (NZ - 1)


def own_shape(shape, kind):
    width = shape["widths"][kind]
    return (NX, NY, NZ, shape["rp"], width) if kind == 2 else (NX, NY, NZ * shape["r"], width)


def ranges():
    return [(c, kind) for c, chunk in enumerate(CHUNKS) for kind in range(3) if chunk[2]["widths"][kind]]


def run_in_slots(stages_of):
    slots = max(c + max(len(s) for s in stages) for c, stages in enumerate(stages_of))
    for slot in range(slots):
        for c in range(len(stages_of) - 1, -1, -1):
            for stages in stages_of[c]:
                if 0 <= slot - c < len(stages):
                    stages[slot - c]()


def reduce_kernel(*refs):
    todo = ranges()
    count = len(todo)
    ins, outs = refs[:count], refs[count : count + len(CHUNKS)]
    rest = list(refs[count + len(CHUNKS) :])
    load, send, recv = rest[:3]
    rest = rest[3:]
    torus = Torus()
    stages_of = [[] for _ in CHUNKS]
    loads = []
    for n, (c, kind) in enumerate(todo):
        _, _, shape, sign, second = CHUNKS[c]
        own = rest.pop(0)
        got = [rest.pop(0) for _ in range(3)]
        loads.append(pltpu.make_async_copy(ins[n], own, load.at[n]))
        start = sum(shape["widths"][:kind])
        out = outs[c].at[:, start : start + shape["widths"][kind]]
        sems = (send, recv, n * HOPS)
        if kind == 2:
            stages = sums_z(torus, second, own, got, out, sign, sems)
        else:
            wide = (rest.pop(0), rest.pop(0))
            pieces = rest.pop(0)
            wide[1][...] = jnp.zeros_like(wide[1])
            axes = ("x", "y") if kind == 0 else ("y", "x")
            stages = sums_xy(torus, *axes, own, got, wide, pieces, out, sign, sems, shape["r"], shape["rp"])
        stages[0] = functools.partial(lambda wait, go: (wait.wait(), go()), loads[-1], stages[0])
        stages_of[c].append(stages)
    for copy in loads:
        copy.start()
    torus.barrier()
    run_in_slots(stages_of)


def reduce_scatter(grads):
    todo = ranges()
    scratch = [
        pltpu.SemaphoreType.DMA((len(todo),)),
        pltpu.SemaphoreType.DMA((len(todo) * HOPS,)),
        pltpu.SemaphoreType.DMA((len(todo) * HOPS,)),
    ]
    for c, kind in todo:
        _, _, shape, _, second = CHUNKS[c]
        r, rp, width = shape["r"], shape["rp"], shape["widths"][kind]
        scratch.append(pltpu.VMEM(own_shape(shape, kind), BF16))
        if kind == 2:
            scratch.append(pltpu.VMEM((NZ - 1, NX, NY, rp, width), BF16))
            n2, n3 = (NX, NY) if second == "x" else (NY, NX)
            scratch.append(pltpu.VMEM((n2 - 1, n3, rp, width), BF16))
            scratch.append(pltpu.VMEM((n3 - 1, rp, width), BF16))
        else:
            n1, n2 = (NX, NY) if kind == 0 else (NY, NX)
            scratch.append(pltpu.VMEM((n1 - 1, n2, NZ * r, width), BF16))
            scratch.append(pltpu.VMEM((n2 - 1, NZ * r, width), BF16))
            scratch.append(pltpu.VMEM((NZ - 1, rp, width), BF16))
            scratch.append(pltpu.VMEM((NZ * r, width), F32))
            scratch.append(pltpu.VMEM((NZ, rp, width), F32))
            scratch.append(pltpu.VMEM((NZ, rp, width), BF16))
    return pl.pallas_call(
        reduce_kernel,
        out_shape=[jax.ShapeDtypeStruct((s["rp"], sum(s["widths"])), BF16) for _, _, s, _, _ in CHUNKS],
        in_specs=[pl.BlockSpec(memory_space=pl.ANY)] * len(todo),
        out_specs=[pl.BlockSpec(memory_space=pltpu.VMEM)] * len(CHUNKS),
        scratch_shapes=scratch,
        compiler_params=pltpu.CompilerParams(collective_id=0, has_side_effects=True, vmem_limit_bytes=67043328),
        name="reduce_scatter",
    )(*grads)


class GatherOver:
    def __init__(self, ring, place):
        self.ring, self.place = ring, place

    def shard(self, flow, hop):
        return self.ring.torus.shifted(self.ring.axis, -self.ring.signs[flow] * hop)

    def step(self, hop, src=None):
        for flow in (0, 1):
            if hop > self.ring.hops[flow]:
                continue
            place = self.place(self.shard(flow, hop))
            if hop:
                self.ring.copy(flow, hop, place, place).wait_recv()
            if hop < self.ring.hops[flow]:
                self.ring.start(flow, hop + 1, place if src is None else src, place)


def gathers_xy(torus, first, second, own, small, flat, place, sign, sems, r):
    me = torus.me
    send, recv, base = sems
    n1, n2 = torus.size[first], torus.size[second]
    rings = (
        Ring(torus, "z", sign, send, recv, base),
        Ring(torus, second, sign, send, recv, base + NZ - 1),
        Ring(torus, first, sign, send, recv, base + NZ + n2 - 2),
    )
    one = GatherOver(rings[0], lambda k: small.at[k])
    if first == "x":
        two = GatherOver(rings[1], lambda j: place.at[me["x"], j])
        three = GatherOver(rings[2], lambda i: place.at[i])
    else:
        two = GatherOver(rings[1], lambda i: place.at[i, me["y"]])
        three = GatherOver(rings[2], lambda j: place.at[:, j])

    def first_start():
        small[me["z"]] = own[...]
        one.step(0, src=own)

    def second_start():
        one.step(NZ // 2)
        for z in range(NZ):
            flat[z * r : (z + 1) * r, :] = small[z].astype(F32)[0:r, :]
        total(place.at[me["x"], me["y"]], [flat])
        two.step(0)

    def third_start():
        two.step(n2 // 2)
        three.step(0)

    def finish():
        three.step(n1 // 2)
        for ring in rings:
            ring.drain()

    stages = [first_start]
    stages += [functools.partial(one.step, h) for h in range(1, NZ // 2)]
    stages.append(second_start)
    stages += [functools.partial(two.step, h) for h in range(1, n2 // 2)]
    stages.append(third_start)
    stages += [functools.partial(three.step, h) for h in range(1, n1 // 2)]
    stages.append(finish)
    return stages


def gathers_z(torus, second, own, place, sign, sems):
    me = torus.me
    third = "y" if second == "x" else "x"
    send, recv, base = sems
    n2, n3 = torus.size[second], torus.size[third]
    rings = (
        Ring(torus, third, sign, send, recv, base),
        Ring(torus, second, sign, send, recv, base + n3 - 1),
        Ring(torus, "z", sign, send, recv, base + n3 + n2 - 2),
    )
    if third == "y":
        one = GatherOver(rings[0], lambda j: place.at[me["x"], j, me["z"]])
        two = GatherOver(rings[1], lambda i: place.at[i, :, me["z"]])
    else:
        one = GatherOver(rings[0], lambda i: place.at[i, me["y"], me["z"]])
        two = GatherOver(rings[1], lambda j: place.at[:, j, me["z"]])
    three = GatherOver(rings[2], lambda k: place.at[:, :, k])

    def first_start():
        place[me["x"], me["y"], me["z"]] = own[...]
        one.step(0, src=own)

    def second_start():
        one.step(n3 // 2)
        two.step(0)

    def third_start():
        two.step(n2 // 2)
        three.step(0)

    def finish():
        three.step(NZ // 2)
        for ring in rings:
            ring.drain()

    stages = [first_start]
    stages += [functools.partial(one.step, h) for h in range(1, n3 // 2)]
    stages.append(second_start)
    stages += [functools.partial(two.step, h) for h in range(1, n2 // 2)]
    stages.append(third_start)
    stages += [functools.partial(three.step, h) for h in range(1, NZ // 2)]
    stages.append(finish)
    return stages


def gather_kernel(*refs):
    todo = ranges()
    count = len(todo)
    ins, outs = refs[: len(CHUNKS)], refs[len(CHUNKS) : len(CHUNKS) + count]
    rest = list(refs[len(CHUNKS) + count :])
    store, send, recv = rest[:3]
    rest = rest[3:]
    torus = Torus()
    stages_of = [[] for _ in CHUNKS]
    stores = []
    for n, (c, kind) in enumerate(todo):
        _, _, shape, sign, second = CHUNKS[c]
        place = rest.pop(0)
        start = sum(shape["widths"][:kind])
        own = ins[c].at[:, start : start + shape["widths"][kind]]
        sems = (send, recv, n * HOPS)
        if kind == 2:
            stages = gathers_z(torus, second, own, place, sign, sems)
        else:
            axes = ("x", "y") if kind == 0 else ("y", "x")
            stages = gathers_xy(torus, *axes, own, rest.pop(0), rest.pop(0), place, sign, sems, shape["r"])
        stores.append(pltpu.make_async_copy(place, outs[n], store.at[n]))
        stages[-1] = functools.partial(lambda go, put: (go(), put.start()), stages[-1], stores[-1])
        stages_of[c].append(stages)
    torus.barrier()
    run_in_slots(stages_of)
    for copy in stores:
        copy.wait()


def all_gather(blocks):
    todo = ranges()
    scratch = [
        pltpu.SemaphoreType.DMA((len(todo),)),
        pltpu.SemaphoreType.DMA((len(todo) * HOPS,)),
        pltpu.SemaphoreType.DMA((len(todo) * HOPS,)),
    ]
    outs = []
    for c, kind in todo:
        shape = CHUNKS[c][2]
        scratch.append(pltpu.VMEM(own_shape(shape, kind), BF16))
        if kind != 2:
            scratch.append(pltpu.VMEM((NZ, shape["rp"], shape["widths"][kind]), BF16))
            scratch.append(pltpu.VMEM((NZ * shape["r"], shape["widths"][kind]), F32))
        outs.append(jax.ShapeDtypeStruct(own_shape(shape, kind), BF16))
    return pl.pallas_call(
        gather_kernel,
        out_shape=outs,
        in_specs=[pl.BlockSpec(memory_space=pltpu.VMEM)] * len(CHUNKS),
        out_specs=[pl.BlockSpec(memory_space=pl.ANY)] * len(todo),
        scratch_shapes=scratch,
        compiler_params=pltpu.CompilerParams(collective_id=1, has_side_effects=True, vmem_limit_bytes=67043328),
        name="all_gather",
    )(*blocks)


def unpack_kernel(r, widths, *refs):
    *ins, out, flat = refs
    per = len(ins) // 2
    layer = pl.program_id(0)
    for l in range(2):

        @pl.when(layer == l)
        def _():
            start = 0
            for kind, ref in enumerate(ins[l * per : (l + 1) * per]):
                width = widths[l][kind]
                if kind < 2:
                    out[0, :, start : start + width] = ref[0, 0]
                else:
                    for z in range(NZ):
                        flat[z * r : (z + 1) * r, :] = ref[0, 0, z].astype(F32)[0:r, :]
                    out[0, :, start : start + width] = flat[...].astype(BF16)
                start += width


def unpack(shapes, layers):
    r = shapes[0]["r"]
    columns = sum(shapes[0]["widths"])
    widths = [s["widths"] for s in shapes]
    specs = []
    for l in range(2):
        for kind in range(3):
            if not widths[l][kind]:
                continue
            if l == 0:
                at = lambda layer, p: jnp.where(layer == 0, p, NX * NY - 1)
            else:
                at = lambda layer, p: jnp.where(layer == 1, p, 0)
            if kind == 2:
                block = (1, 1, NZ, shapes[l]["rp"], widths[l][2])
                specs.append(pl.BlockSpec(block, lambda layer, p, at=at: (at(layer, p) // NY, at(layer, p) % NY, 0, 0, 0)))
            else:
                block = (1, 1, NZ * r, widths[l][kind])
                specs.append(pl.BlockSpec(block, lambda layer, p, at=at: (at(layer, p) // NY, at(layer, p) % NY, 0, 0)))
    return pl.pallas_call(
        functools.partial(unpack_kernel, r, widths),
        grid=(2, NX * NY),
        out_shape=jax.ShapeDtypeStruct((2, NX * NY * NZ * r, columns), BF16),
        in_specs=specs,
        out_specs=pl.BlockSpec((1, NZ * r, columns), lambda layer, p: (layer, p, 0)),
        scratch_shapes=[pltpu.VMEM((NZ * r, max(widths[0][2], 128)), F32)],
        name="unpack",
    )(*layers[0], *layers[1])


def dot(a, b, contract=((1,), (0,))):
    return lax.dot_general(a, b, (contract, ((), ())), preferred_element_type=F32)


def normed(h):
    wide = h.astype(F32)
    scale = lax.rsqrt(jnp.mean(wide**2, -1, keepdims=True) + 1e-6)
    return (wide * scale).astype(BF16), scale


def through(ct, gate, up, w_down):
    by_hidden = dot(ct, w_down, ((1,), (1,))).astype(BF16).astype(F32)
    sig = jax.nn.sigmoid(gate)
    silu = gate * sig
    by_gate = by_hidden * up * (sig * (1 + gate * (1 - sig)))
    return by_gate.astype(BF16), (by_hidden * silu).astype(BF16)


def local_gradients(x, dy, weights):
    w_gate, w_up, w_down = weights
    spread = (jnp.arange(D)[:, None] // 7 * 8 + jnp.arange(D)[:, None] % 7 == jnp.arange(D // 7 * 8)[None, :]).astype(BF16)

    def up_to_hidden(h, l):
        a, scale = normed(h)
        gate, up = dot(a, w_gate[l]), dot(a, w_up[l])
        return a, scale, gate, up, (jax.nn.silu(gate) * up).astype(BF16)

    a0, _, gate0, up0, hidden0 = up_to_hidden(x, 0)
    h1 = x + dot(hidden0, w_down[0]).astype(BF16)
    a1, scale1, gate1, up1, hidden1 = up_to_hidden(h1, 1)
    by_gate1, by_up1 = through(dy, gate1, up1, w_down[1])
    by_a = (dot(by_gate1, w_gate[1], ((1,), (1,))) + dot(by_up1, w_up[1], ((1,), (1,)))).astype(BF16).astype(F32)
    wide = h1.astype(F32)
    inner = jnp.mean(by_a * wide, -1, keepdims=True)
    by_h = dy + (by_a * scale1 - wide * (scale1**3 * inner)).astype(BF16)
    by_gate0, by_up0 = through(by_h, gate0, up0, w_down[0])
    grads = []
    for name, l, shape, _, _ in CHUNKS:
        widths = shape["widths"]
        if name == "w_down":
            hidden, ct = ((hidden0, by_h), (hidden1, dy))[l]
            g = dot(hidden, ct, ((0,), (0,))).astype(BF16)
            parts = [g[:, : widths[0]], g[:, widths[0] :]]
        else:
            a = (a0, a1)[l]
            by = ((by_gate0, by_up0), (by_gate1, by_up1))[l][name == "w_up"]
            g = dot(a, by[:, : widths[0] + widths[1]], ((0,), (0,))).astype(BF16)
            a_spread = dot(a, spread).astype(BF16)
            gz = dot(a_spread, by[:, widths[0] + widths[1] :], ((0,), (0,))).astype(BF16)
            parts = [g[:, : widths[0]], g[:, widths[0] :], gz]
        grads += [part.reshape(own_shape(shape, kind)) for kind, part in enumerate(parts)]
    return grads


def adamw(w, m, v, g):
    m = 0.9 * m + 0.1 * g
    v = 0.95 * v + 0.05 * g * g
    step = m * lax.rsqrt(v + 1e-8) + 0.1 * w
    return (w - 0.02 * step).astype(BF16), m, v


NAMES = ("w_gate", "w_up", "w_down")


def solution(mesh):
    def step(x, dy, *arrays):
        weights, ms, vs = (arrays[i : i + 3] for i in (0, 3, 6))
        sums = reduce_scatter(local_gradients(x[0], dy[0], weights))
        dp = lax.axis_index("dp")
        blocks, new_m, new_v = {}, {}, {}
        for (name, l, shape, _, _), g in zip(CHUNKS, sums, strict=True):
            n, r = NAMES.index(name), shape["r"]
            w = lax.dynamic_slice_in_dim(weights[n][l], dp * r, r, 0)
            w, m, v = adamw(w.astype(F32), ms[n][l], vs[n][l], g[:r].astype(F32))
            blocks[name, l] = jnp.pad(w, ((0, shape["rp"] - r), (0, 0)))
            new_m[name, l], new_v[name, l] = m, v
        gathered = list(all_gather([blocks[name, l] for name, l, *_ in CHUNKS]))
        layers = {}
        for name, l, shape, _, _ in CHUNKS:
            layers[name, l] = [gathered.pop(0) for width in shape["widths"] if width]
        shapes = {(name, l): shape for name, l, shape, _, _ in CHUNKS}
        new_w = [unpack([shapes[n, 0], shapes[n, 1]], [layers[n, 0], layers[n, 1]]) for n in NAMES]
        return (
            *new_w,
            *(jnp.stack([new_m[n, 0], new_m[n, 1]]) for n in NAMES),
            *(jnp.stack([new_v[n, 0], new_v[n, 1]]) for n in NAMES),
        )

    batch, whole, rows = P(("rep", "dp")), P(), P(None, "dp")
    return jax.shard_map(
        step,
        mesh=mesh,
        in_specs=(batch, batch, *[whole] * 3, *[rows] * 6),
        out_specs=(*[P("rep")] * 3, *[P("rep", "dp")] * 6),
        check_vma=False,
    )
```

time: 2200 us -> 710 us (0.32)
  blocking collectives: 1260 us -> 0 us
  Pallas kernels: 0 us -> 338 us
  waiting for transfers between devices: 272 us -> 0 us
  starting transfers between devices: 237 us -> 0 us
  other arithmetic: 51.9 us -> 14.8 us
    unnamed x2 -> x0, blocking collectives: 1260 us -> none
    pallas_call x0 -> x5, Pallas kernels: none -> 338 us  [the longest x1 149 us: reduce_scatter(): pl.pallas_call(reduce_kernel, out_shape=[jax.ShapeDtypeStruct((s['rp'], s...]
    unnamed x64 -> x0, starting transfers between devices: 237 us -> none
    reshape x3 -> x0, waiting for transfers between devices: 233 us -> none  [step(): t.reshape(-1, *t.shape[2:])]
    unnamed x108 -> x110, local copies, waits for them, and re-layouts: 76.7 us -> 17.9 us
    unnamed x8 -> x5, other arithmetic: 45 us -> 0.01 us
    slice x0 -> x17, local copies, waits for them, and re-layouts: none -> 40.2 us  [the longest x2 12.3 us: up_to_hidden(): gate, up = (dot(a, w_gate[l]), dot(a, w_up[l]))]
    unnamed x67 -> x0, waiting for transfers between devices: 38.8 us -> none
  transfers between devices with their start and end apart: 67 -> 0, of which waited for: 10 -> 0; matrix products, arithmetic and copies ran while one was open for 30% -> 0% of each run, Pallas kernels for 0% -> 0%
where the time goes in v1:
time: 710 us; the launch traced here: 700 us
  Pallas kernels  338 us (48%)
  matrix products  284 us (40%)
  local copies, waits for them, and re-layouts  61.8 us (9%)
  other arithmetic  14.8 us (2%)
    dot_general x21, matrix products, dot(): lax.dot_general(a, b, (contract, ((), ())), preferred_element_type=F32)  284 us
    pallas_call x1, Pallas kernels, reduce_scatter(): pl.pallas_call(reduce_kernel, out_shape=[jax.ShapeDtypeStruct((s['rp'], s...  149 us
    pallas_call x1, Pallas kernels, all_gather(): pl.pallas_call(gather_kernel, out_shape=outs, in_specs=[pl.BlockSpec(memo...  127 us
    pallas_call x3, Pallas kernels, unpack(): pl.pallas_call(functools.partial(unpack_kernel, r, widths), grid=(2, NX *...  61.6 us
    unnamed x110, local copies, waits for them, and re-layouts  17.9 us

profile of v1, /device:TPU:2, one launch (start us, length us, event | category | flops | bytes accessed | tf_op | source)
XLA Modules:
  0.0 700.2 jit_solution(7158366368596561412)
XLA Ops:
  2.4 6.0 copy.21
  11.3 18.3 %fusion.43 = f32[2048,2560]{1,0:T(8,128)} fusion(bf16[1,2048,896]{2,1,0:T(8,128)(2,1)} %param.11, f32[2048]{0:T(1024)S(1)} %add_rsqrt_fusion.1, bf16[2,896,2560]{2,1,0:T(8,128)(2,1)} %param.13), kind=kOutput, calls=%fused_computation.63 | convolution fusion | flops 9400745984 | bytes 29237248 | tf_op jit(solution)/shard_map/dot_general | solution.py:581
  29.6 24.5 %multiply_convert_fusion.1 = (bf16[2048,2560]{1,0:T(8,128)(2,1)}, f32[2048,2560]{1,0:T(8,128)}) fusion(f32[2048,2560]{1,0:T(8,128)} %fusion.43, bf16[2,896,2560]{2,1,0:T(8,128)(2,1)} %param.14, bf16[1,2048,896]{2,1,0:T(8,128)(2,1)S(1)} %copy-done.2, f32[2048]{0:T(1024)S(1)} %add_rsqrt_fusion.1), kind=kOutput, calls=%fused_computation.13 | convolution fusion | flops 9432203264 | bytes 60694528 | tf_op jit(solution)/shard_map/dot_general | solution.py:581
  54.1 14.8 %fusion.13 = (f32[2048]{0:T(1024)S(1)}, bf16[2048,896]{0,1:T(8,128)(2,1)S(1)}) fusion(bf16[2048,2560]{1,0:T(8,128)(2,1)} %get-tuple-element.110, bf16[2,2560,896]{2,1,0:T(8,128)(2,1)} %param.15, bf16[1,2048,896]{1,2,0:T(8,128)(2,1)S(1)} %copy-done), kind=kOutput, calls=%fused_computation.30 | convolution fusion | flops 9404413952 | bytes 22421504 | tf_op jit(solution)/shard_map/dot_general | solution.py:581
  68.9 18.4 %fusion.32 = f32[2048,2560]{1,0:T(8,128)} fusion(bf16[2048,896]{0,1:T(8,128)(2,1)S(1)} %get-tuple-element.113, f32[2048]{0:T(1024)S(1)} %add_rsqrt_fusion, bf16[2,896,2560]{2,1,0:T(8,128)(2,1)} %param.14), kind=kOutput, calls=%fused_computation.52 | convolution fusion | flops 9400745984 | bytes 29237248 | tf_op jit(solution)/shard_map/dot_general | solution.py:581
  87.4 17.5 %fusion.36 = f32[2048,2560]{1,0:T(8,128)} fusion(bf16[2048,896]{0,1:T(8,128)(2,1)S(1)} %get-tuple-element.113, f32[2048]{0:T(1024)S(1)} %add_rsqrt_fusion, bf16[2,896,2560]{2,1,0:T(8,128)(2,1)} %param.13), kind=kOutput, calls=%fused_computation.56 | convolution fusion | flops 9400745984 | bytes 29237248 | tf_op jit(solution)/shard_map/dot_general | solution.py:581
  104.8 21.5 %fusion.20 = bf16[2560,896]{1,0:T(8,128)(2,1)} fusion(f32[2048,2560]{1,0:T(8,128)} %fusion.32, bf16[1,2048,896]{2,1,0:T(8,128)(2,1)} %param.12, f32[2048,2560]{1,0:T(8,128)} %fusion.36), kind=kOutput, calls=%fused_computation.39 | convolution fusion | flops 9428992000 | bytes 50200576 | tf_op jit(solution)/shard_map/dot_general | solution.py:581
  132.9 28.4 %fusion.2 = (bf16[2048,2560]{1,0:T(8,128)(2,1)}, bf16[2048,2560]{1,0:T(8,128)(2,1)}) fusion(f32[2048,2560]{1,0:T(8,128)} %fusion.36, f32[2048,2560]{1,0:T(8,128)} %fusion.32, bf16[2,2560,896]{2,1,0:T(8,128)(2,1)} %param.15, bf16[1,2048,896]{2,1,0:T(8,128)(2,1)S(1)} %copy-done.3), kind=kOutput, calls=%fused_computation.6 | convolution fusion | flops 9473884160 | bytes 71172096 | tf_op jit(solution)/shard_map/dot_general | solution.py:581
  161.3 7.6 %fusion.64 = bf16[896,1280]{1,0:T(8,128)(2,1)S(1)} fusion(bf16[2048,2560]{1,0:T(8,128)(2,1)} %get-tuple-element.65, bf16[2048,896]{0,1:T(8,128)(2,1)S(1)} %copy-done.5, f32[2048]{0:T(1024)S(1)} %add_rsqrt_fusion), kind=kOutput, calls=%fused_computation.79 | convolution fusion | flops 4704272384 | bytes 11214848 | tf_op jit(solution)/shard_map/dot_general | solution.py:581
  171.1 5.0 convolution_convert_fusion.4
  176.2 7.1 %fusion.49 = bf16[1024,1280]{1,0:T(8,128)(2,1)} fusion(bf16[2048,1024]{1,0:T(8,128)(2,1)S(1)} %convolution_convert_fusion.4, bf16[2048,2560]{1,0:T(8,128)(2,1)S(1)} %bitcast.250), kind=kOutput, calls=%fused_computation.69 | convolution fusion | flops 5370019840 | bytes 12058624 | tf_op jit(solution)/shard_map/dot_general | solution.py:581
  183.3 6.3 fusion.70
  191.4 8.5 %fusion.84 = bf16[1024,1024]{1,0:T(8,128)(2,1)} fusion(bf16[2048,1024]{1,0:T(8,128)(2,1)S(1)} %convolution_convert_fusion.4, bf16[2048,2560]{1,0:T(8,128)(2,1)} %get-tuple-element.64), kind=kOutput, calls=%fused_computation.83 | convolution fusion | flops 4296015872 | bytes 10485760 | tf_op jit(solution)/shard_map/dot_general | solution.py:581
  199.9 14.3 %fusion.30 = f32[2048,896]{0,1:T(8,128)} fusion(bf16[2048,2560]{1,0:T(8,128)(2,1)} %get-tuple-element.64, bf16[2,896,2560]{2,1,0:T(8,128)(2,1)S(1)} %bitcast.228), kind=kOutput, calls=%fused_computation.50 | convolution fusion | flops 9395240960 | bytes 22413312 | tf_op jit(solution)/shard_map/dot_general | solution.py:581
  214.2 14.9 %fusion.15 = (f32[2048]{0:T(1024)S(1)}, bf16[2048,896]{0,1:T(8,128)(2,1)}) fusion(bf16[2048,896]{0,1:T(8,128)(2,1)S(1)} %copy-done.5, f32[2048,896]{0,1:T(8,128)} %fusion.30, bf16[2048,2560]{1,0:T(8,128)(2,1)} %get-tuple-element.65, bf16[2,896,2560]{2,1,0:T(8,128)(2,1)S(1)} %bitcast.230), kind=kOutput, calls=%fused_computation.32 | convolution fusion | flops 9406248960 | bytes 29761536 | tf_op jit(solution)/shard_map/dot_general | solution.py:581
  229.2 6.4 copy.22
  235.7 6.8 fusion.56
  242.5 13.9 %convolution_convert_fusion.2 = bf16[2560,896]{1,0:T(8,128)(2,1)S(1)} fusion(bf16[2048,2560]{1,0:T(8,128)(2,1)} %get-tuple-element.110, bf16[2048,896]{0,1:T(8,128)(2,1)S(1)} %fusion.56), kind=kOutput, calls=%fused_computation.40 | convolution fusion | flops 9397534720 | bytes 18743296 | tf_op jit(solution)/shard_map/dot_general | solution.py:581
  259.6 28.6 %fusion.5 = (bf16[2048,2560]{1,0:T(8,128)(2,1)}, bf16[2048,2560]{1,0:T(8,128)(2,1)}) fusion(f32[2048,2560]{1,0:T(8,128)} %fusion.43, f32[2048,2560]{1,0:T(8,128)} %get-tuple-element.111, bf16[2048,896]{0,1:T(8,128)(2,1)S(1)} %fusion.56, bf16[2,2560,896]{2,1,0:T(8,128)(2,1)} %param.15), kind=kOutput, calls=%fused_computation.9 | convolution fusion | flops 9473884160 | bytes 71172096 | tf_op jit(solution)/shard_map/dot_general | solution.py:581
  288.2 7.6 %fusion.67 = bf16[896,1280]{1,0:T(8,128)(2,1)S(1)} fusion(bf16[2048,2560]{1,0:T(8,128)(2,1)} %get-tuple-element.63, bf16[1,2048,896]{1,2,0:T(8,128)(2,1)S(1)} %copy-done.1, f32[2048]{0:T(1024)S(1)} %copy-done.33), kind=kOutput, calls=%fused_computation.80 | convolution fusion | flops 4704272384 | bytes 11214848 | tf_op jit(solution)/shard_map/dot_general | solution.py:581
  297.6 5.1 convolution_convert_fusion.3
  302.7 9.7 %fusion.52 = bf16[1024,1280]{1,0:T(8,128)(2,1)} fusion(bf16[2048,1024]{1,0:T(8,128)(2,1)S(1)} %convolution_convert_fusion.3, bf16[2048,2560]{1,0:T(8,128)(2,1)} %get-tuple-element.63), kind=kOutput, calls=%fused_computation.70 | convolution fusion | flops 5370019840 | bytes 12058624 | tf_op jit(solution)/shard_map/dot_general | solution.py:581
  312.4 6.3 fusion.73
  320.5 5.7 fusion.87
  326.2 149.4 %reduce_scatter.1 = (bf16[24,896]{1,0:T(8,128)(2,1)}, bf16[8,2560]{1,0:T(8,128)(2,1)}, bf16[8,2560]{1,0:T(8,128)(2,1)}, bf16[24,896]{1,0:T(8,128)(2,1)}, bf16[8,...) custom-call(bf16[4,4,160,512]{3,2,1,0:T(8,128)(2,1)} %bitcast.225, bf16[4,4,160,384]{3,2,1,0:T(8,128)(2,1)} %bitcast.231, ...), custom_call_target="tpu_custom_call" | custom-call | tf_op jit(solution)/shard_map/reduce_scatter/pallas_call | solution.py:353
  476.8 8.2 %fusion.170 = (bf16[1,2560,896]{2,1,0:T(8,128)(2,1)}, bf16[1,2560,896]{2,1,0:T(8,128)(2,1)}) fusion(bf16[2,2560,896]{2,1,0:T(8,128)(2,1)} %param.15), kind=kLoop, calls=%fused_computation.212 | loop fusion | bytes 18350080 | tf_op jit(solution)/shard_map/slice | solution.py:608
  487.5 8.0 %fusion.168 = (bf16[1,896,2560]{2,1,0:T(8,128)(2,1)}, bf16[1,896,2560]{2,1,0:T(8,128)(2,1)}) fusion(bf16[2,896,2560]{2,1,0:T(8,128)(2,1)} %param.14), kind=kLoop, calls=%fused_computation.210 | loop fusion | bytes 18350080 | tf_op jit(solution)/shard_map/slice | solution.py:604
  495.8 4.3 fusion.169
  506.6 126.7 %all_gather.1 = (bf16[4,4,160,512]{3,2,1,0:T(8,128)(2,1)}, bf16[4,4,160,384]{3,2,1,0:T(8,128)(2,1)}, bf16[4,4,56,640]{3,2,1,0:T(8,128)(2,1)}, bf16[4,4,56,640]{3...) custom-call(bf16[24,896]{1,0:T(8,128)(2,1)} %pad.20.refs_0_, ...), custom_call_target="tpu_custom_call" | custom-call | tf_op jit(solution)/shard_map/all_gather/pallas_call | solution.py:519
  633.3 20.7 %unpack.3 = bf16[2,896,2560]{2,1,0:T(8,128)(2,1)} custom-call(bf16[4,4,56,640]{3,2,1,0:T(8,128)(2,1)} %get-tuple-element.37.refs_0_, bf16[4,4,56,640]{3,2,1,0:T(8,128)(2,1)} %get-tuple-element.38.refs_1_, bf16[4,4,8,8,1280]{4,3,2,1,0:T(8,128)(2,1)} %get-tuple-element.39.refs_2_, bf16[4,4,56,640]{3,2,1,0:T(8,128)(2,1)} %get-tuple-element.40.refs_3_, ...), custom_call_target="tpu_custom_call" | custom-call | tf_op jit(solution)/shard_map/unpack/pallas_call | solution.py:569
  654.1 20.6 %unpack.4 = bf16[2,896,2560]{2,1,0:T(8,128)(2,1)} custom-call(bf16[4,4,56,768]{3,2,1,0:T(8,128)(2,1)} %get-tuple-element.43.refs_0_, bf16[4,4,56,768]{3,2,1,0:T(8,128)(2,1)} %get-tuple-element.44.refs_1_, bf16[4,4,8,8,1024]{4,3,2,1,0:T(8,128)(2,1)} %get-tuple-element.45.refs_2_, bf16[4,4,56,768]{3,2,1,0:T(8,128)(2,1)} %get-tuple-element.46.refs_3_, ...), custom_call_target="tpu_custom_call" | custom-call | tf_op jit(solution)/shard_map/unpack/pallas_call | solution.py:569
  674.8 20.3 %unpack.5 = bf16[2,2560,896]{2,1,0:T(8,128)(2,1)} custom-call(bf16[4,4,160,384]{3,2,1,0:T(8,128)(2,1)} %get-tuple-element.49.refs_0_, bf16[4,4,160,512]{3,2,1,0:T(8,128)(2,1)} %get-tuple-element.50.refs_1_, bf16[4,4,160,512]{3,2,1,0:T(8,128)(2,1)} %get-tuple-element.51.refs_2_, bf16[4,4,160,384]{3,2,1,0:T(8,128)(2,1)} %get-tuple-element.52.refs_3_), custom_call_target="tpu_custom_call" | custom-call | tf_op jit(solution)/shard_map/unpack/pallas_call | solution.py:569
  (147 shorter events, 36.9 us)
Async XLA Ops:
  11.3 18.3 %copy-start.32 = (f32[2048]{0:T(1024)}, f32[2048]{0:T(1024)S(1)}, u32[]{:S(2)}) copy-start(f32[2048]{0:T(1024)S(1)} %add_rsqrt_fusion.1) | copy-start | bytes 24580
  11.3 18.3 %copy-start.2 = (bf16[1,2048,896]{2,1,0:T(8,128)(2,1)S(1)}, bf16[1,2048,896]{2,1,0:T(8,128)(2,1)}, u32[]{:S(2)}) copy-start(bf16[1,2048,896]{2,1,0:T(8,128)(2,1)} %param.11) | copy-start | bytes 11010052
  29.6 24.5 %copy-start = (bf16[1,2048,896]{1,2,0:T(8,128)(2,1)S(1)}, bf16[1,2048,896]{1,2,0:T(8,128)(2,1)}, u32[]{:S(2)}) copy-start(bf16[1,2048,896]{1,2,0:T(8,128)(2,1)} %copy.21) | copy-start | bytes 11010052
  68.9 18.5 %copy-start.4 = (bf16[2048,896]{0,1:T(8,128)(2,1)}, bf16[2048,896]{0,1:T(8,128)(2,1)S(1)}, u32[]{:S(2)}) copy-start(bf16[2048,896]{0,1:T(8,128)(2,1)S(1)} %get-tuple-element.113) | copy-start | bytes 11010052
  68.9 18.5 %copy-start.30 = (f32[2048]{0:T(1024)}, f32[2048]{0:T(1024)S(1)}, u32[]{:S(2)}) copy-start(f32[2048]{0:T(1024)S(1)} %get-tuple-element.112) | copy-start | bytes 24580
  132.9 28.5 %copy-start.5 = (bf16[2048,896]{0,1:T(8,128)(2,1)S(1)}, bf16[2048,896]{0,1:T(8,128)(2,1)}, u32[]{:S(2)}) copy-start(bf16[2048,896]{0,1:T(8,128)(2,1)} %copy-done.4) | copy-start | bytes 11010052
  171.1 12.2 %slice-start.9 = ((s8[10485760]{0:T(1024)(128)(4,1)}), s8[4194304]{0:T(1024)(128)(4,1)S(1)}, s32[]{:S(2)}) async-start(s8[10485760]{0:T(1024)(128)(4,1)} %bitcast.247), calls=%async_computation.9 | async-start | bytes 8388608
  171.1 12.2 %slice-start.10 = ((s8[10485760]{0:T(1024)(128)(4,1)}), s8[4194304]{0:T(1024)(128)(4,1)S(1)}, s32[]{:S(2)}) async-start(s8[10485760]{0:T(1024)(128)(4,1)} %bitcast.247), calls=%async_computation.10 | async-start | bytes 8388608
  189.6 10.2 %slice-start = ((s8[9175040]{0:T(1024)(128)(4,1)}), s8[4194304]{0:T(1024)(128)(4,1)S(1)}, s32[]{:S(2)}) async-start(s8[9175040]{0:T(1024)(128)(4,1)} %bitcast.227), calls=%async_computation | async-start | bytes 8388608
  191.4 22.9 %slice-start.3 = ((s8[9175040]{0:T(1024)(128)(4,1)}), s8[4194304]{0:T(1024)(128)(4,1)S(1)}, s32[]{:S(2)}) async-start(s8[9175040]{0:T(1024)(128)(4,1)} %bitcast.229), calls=%async_computation.3 | async-start | bytes 8388608
  199.9 14.4 %slice-start.4 = ((s8[9175040]{0:T(1024)(128)(4,1)}), s8[4194304]{0:T(1024)(128)(4,1)S(1)}, s32[]{:S(2)}) async-start(s8[9175040]{0:T(1024)(128)(4,1)} %bitcast.229), calls=%async_computation.4 | async-start | bytes 8388608
  199.9 14.4 %slice-start.5 = ((s8[9175040]{0:T(1024)(128)(4,1)}), s8[786432]{0:T(1024)(128)(4,1)S(1)}, s32[]{:S(2)}) async-start(s8[9175040]{0:T(1024)(128)(4,1)} %bitcast.229), calls=%async_computation.5 | async-start | bytes 1572864
  259.6 28.6 %copy-start.1 = (bf16[1,2048,896]{1,2,0:T(8,128)(2,1)S(1)}, bf16[1,2048,896]{1,2,0:T(8,128)(2,1)}, u32[]{:S(2)}) copy-start(bf16[1,2048,896]{1,2,0:T(8,128)(2,1)} %copy.21) | copy-start | bytes 11010052
  259.6 28.6 %copy-start.33 = (f32[2048]{0:T(1024)S(1)}, f32[2048]{0:T(1024)}, u32[]{:S(2)}) copy-start(f32[2048]{0:T(1024)} %copy-done.32) | copy-start | bytes 24580
  288.2 9.4 %copy-start.35 = (s32[896]{0:T(1024)S(1)}, s32[896]{0:T(1024)}, u32[]{:S(2)}) copy-start(s32[896]{0:T(1024)} %copy-done.34) | copy-start | bytes 10756
  297.6 14.8 %slice-start.6 = ((s8[10485760]{0:T(1024)(128)(4,1)}), s8[4194304]{0:T(1024)(128)(4,1)S(1)}, s32[]{:S(2)}) async-start(s8[10485760]{0:T(1024)(128)(4,1)} %bitcast.245), calls=%async_computation.6 | async-start | bytes 8388608
  297.6 14.8 %slice-start.7 = ((s8[10485760]{0:T(1024)(128)(4,1)}), s8[4194304]{0:T(1024)(128)(4,1)S(1)}, s32[]{:S(2)}) async-start(s8[10485760]{0:T(1024)(128)(4,1)} %bitcast.245), calls=%async_computation.7 | async-start | bytes 8388608
  302.7 9.7 %slice-start.8 = ((s8[10485760]{0:T(1024)(128)(4,1)}), s8[2097152]{0:T(1024)(128)(4,1)S(1)}, s32[]{:S(2)}) async-start(s8[10485760]{0:T(1024)(128)(4,1)} %bitcast.245), calls=%async_computation.8 | async-start | bytes 4194304
  476.8 10.5 %copy-start.20 = (f32[2,7,2560]{2,0,1:T(2,128)S(1)}, f32[2,7,2560]{2,0,1:T(2,128)}, u32[]{:S(2)}) copy-start(f32[2,7,2560]{2,0,1:T(2,128)} %param.20) | copy-start | bytes 430084
  476.8 10.6 %copy-start.21 = (f32[2,7,2560]{2,0,1:T(2,128)S(1)}, f32[2,7,2560]{2,0,1:T(2,128)}, u32[]{:S(2)}) copy-start(f32[2,7,2560]{2,0,1:T(2,128)} %param.17) | copy-start | bytes 430084
  674.7 20.4 %copy-start.13 = (f32[1,7,2560]{2,1,0:T(8,128)S(1)}, f32[1,7,2560]{2,1,0:T(8,128)}, u32[]{:S(2)}) copy-start(f32[1,7,2560]{2,1,0:T(8,128)} %get-tuple-element.122) | copy-start | bytes 215044
  674.7 20.4 %copy-start.17 = (f32[1,7,2560]{2,1,0:T(8,128)S(1)}, f32[1,7,2560]{2,1,0:T(8,128)}, u32[]{:S(2)}) copy-start(f32[1,7,2560]{2,1,0:T(8,128)} %get-tuple-element.119) | copy-start | bytes 215044
  674.7 21.2 %copy-start.12 = (f32[1,7,2560]{2,1,0:T(8,128)S(1)}, f32[1,7,2560]{2,1,0:T(8,128)}, u32[]{:S(2)}) copy-start(f32[1,7,2560]{2,1,0:T(8,128)} %get-tuple-element.103) | copy-start | bytes 215044
  674.7 21.2 %copy-start.16 = (f32[1,7,2560]{2,1,0:T(8,128)S(1)}, f32[1,7,2560]{2,1,0:T(8,128)}, u32[]{:S(2)}) copy-start(f32[1,7,2560]{2,1,0:T(8,128)} %get-tuple-element.100) | copy-start | bytes 215044
  674.7 22.0 %copy-start.8 = (f32[1,20,896]{2,1,0:T(8,128)S(1)}, f32[1,20,896]{2,1,0:T(8,128)}, u32[]{:S(2)}) copy-start(f32[1,20,896]{2,1,0:T(8,128)} %get-tuple-element.94) | copy-start | bytes 215044
  674.7 22.0 %copy-start.9 = (f32[1,20,896]{2,1,0:T(8,128)S(1)}, f32[1,20,896]{2,1,0:T(8,128)}, u32[]{:S(2)}) copy-start(f32[1,20,896]{2,1,0:T(8,128)} %get-tuple-element.116) | copy-start | bytes 215044
  674.7 22.7 %copy-start.11 = (f32[1,7,2560]{2,1,0:T(8,128)S(1)}, f32[1,7,2560]{2,1,0:T(8,128)}, u32[]{:S(2)}) copy-start(f32[1,7,2560]{2,1,0:T(8,128)} %get-tuple-element.124) | copy-start | bytes 215044
  674.7 22.7 %copy-start.15 = (f32[1,7,2560]{2,1,0:T(8,128)S(1)}, f32[1,7,2560]{2,1,0:T(8,128)}, u32[]{:S(2)}) copy-start(f32[1,7,2560]{2,1,0:T(8,128)} %get-tuple-element.121) | copy-start | bytes 215044
  674.8 23.5 %copy-start.10 = (f32[1,7,2560]{2,1,0:T(8,128)S(1)}, f32[1,7,2560]{2,1,0:T(8,128)}, u32[]{:S(2)}) copy-start(f32[1,7,2560]{2,1,0:T(8,128)} %get-tuple-element.101) | copy-start | bytes 215044
  674.8 23.5 %copy-start.14 = (f32[1,7,2560]{2,1,0:T(8,128)S(1)}, f32[1,7,2560]{2,1,0:T(8,128)}, u32[]{:S(2)}) copy-start(f32[1,7,2560]{2,1,0:T(8,128)} %get-tuple-element.98) | copy-start | bytes 215044
  674.8 24.3 %copy-start.6 = (f32[1,20,896]{2,1,0:T(8,128)S(1)}, f32[1,20,896]{2,1,0:T(8,128)}, u32[]{:S(2)}) copy-start(f32[1,20,896]{2,1,0:T(8,128)} %get-tuple-element.92) | copy-start | bytes 215044
  674.8 24.3 %copy-start.7 = (f32[1,20,896]{2,1,0:T(8,128)S(1)}, f32[1,20,896]{2,1,0:T(8,128)}, u32[]{:S(2)}) copy-start(f32[1,20,896]{2,1,0:T(8,128)} %get-tuple-element.118) | copy-start | bytes 215044
  (19 other events, 128.5 us)
